TPU v7x, 128 devices: a whole 4x4x4 slice. The times are simulated.
128 devices in a mesh: ctx: 16 (over x, z), tp: 8 (over y, core).
Axes of the slice: x: 4, y: 4, z: 4, core: 2. Of those that a mesh axis runs over, the one named last changes fastest.
Arguments:
- queries: bfloat16 [512, 8192], P('ctx', 'tp'), may hold values from -6 to 6
- cache_keys: bfloat16 [65536, 1024], P('ctx', 'tp'), may hold values from -18 to 18
- cache_values: bfloat16 [65536, 1024], P('ctx', 'tp'), may hold values from -6 to 6
- span_keys: bfloat16 [512, 1024], P('ctx', 'tp'), may hold values from -24 to 24
- span_values: bfloat16 [512, 1024], P('ctx', 'tp'), may hold values from -6 to 6
- out_weight: bfloat16 [8192, 8192], P('tp', 'ctx'), may hold values from -0.0625 to 0.0625
- residual: bfloat16 [512, 8192], P('tp', 'ctx'), may hold values from -72 to 72
- norm_gain: bfloat16 [8192], P('ctx'), may hold values from 0.5 to 1.5
- head_weight: bfloat16 [8192, 128256], P(None, ('ctx', 'tp')), may hold values from -0.198873782 to 0.198873782
- targets: int32 [512], replicated, may hold values from 0 to 128255
- window_lengths: int32 [8], replicated, may hold values from 1 to 128, 512 in all
Outputs:
- token_logprob: float32 [512], P('ctx')
- window_means: float32 [8], replicated
Inputs may be any that keep to these rules, and one draw needn't show every extreme that they name: `window_lengths`: the 8 lengths sum to 512.
All inputs are finite; a program needn't handle non-finite values.
Results may differ from a plain program's by a relative error of at most 0.0025.
Values may be sent and summed in bfloat16 or wider, within the bound.
No kernel may reach another device: no remote copies, remote signals or barrier semaphores. Data moves between devices by JAX's collectives and lax.ppermute only.
A program may use at most 128 MiB of HBM per device.

v0:
```python
import jax
import jax.numpy as jnp
from jax import lax
from jax.sharding import Mesh
from jax.sharding import PartitionSpec as P

D = 8192
HEADS = 64
KV_HEADS = 8
HD = 128
CTX = ("ctx_0", "ctx_1")
TP = ("tp_0", "tp_1")
CTX_TP = ("ctx_0", "ctx_1", "tp_0", "tp_1")


EPSILON = 1e-05
NEGATIVE = -1e30


def in_order(blocks, dim):
    blocks = jnp.moveaxis(blocks, 0, dim)
    shape = blocks.shape
    return blocks.reshape(*shape[:dim], shape[dim] * shape[dim + 1], *shape[dim + 2 :])


def sent_to_all(value, axis):
    count = lax.axis_size(axis)
    return lax.all_to_all(
        jnp.broadcast_to(value[None], (count, *value.shape)), axis, 0, 0, tiled=True
    )


def gathered_copies(value, axis, dim):
    return in_order(sent_to_all(value, axis), dim)


def sent_together(arrays, axis, split_dim, concat_dim, along):
    ends, at = ([], 0)
    for a in arrays[:-1]:
        at += a.shape[along]
        ends.append(at)
    both = jnp.concatenate(arrays, axis=along)
    return tuple(
        jnp.split(
            lax.all_to_all(both, axis, split_axis=split_dim, concat_axis=concat_dim, tiled=True),
            ends,
            axis=along,
        )
    )


def in_blocks(value, dim, count):
    shape = value.shape
    blocks = value.reshape(*shape[:dim], count, shape[dim] // count, *shape[dim + 1 :])
    return jnp.moveaxis(blocks, dim, 0)


def summed_on_arrival(value, axis, dim):
    blocks = in_blocks(value, dim, lax.axis_size(axis))
    arrived = lax.all_to_all(blocks, axis, split_axis=0, concat_axis=0, tiled=True)
    return arrived.astype(jnp.float32).sum(axis=0)


def over_axes(value, axes):
    for axis in axes:
        value = lax.psum(value, axis)
    return value


def gathered_once(value, axis):
    leaves = jax.tree.leaves(value)
    order = sorted(range(len(leaves)), key=lambda k: -leaves[k].size)
    width = (1, *leaves[order[0]].shape)[-1]
    lines = [
        jnp.pad(leaves[k].reshape(-1), (0, -leaves[k].size % width)).reshape(-1, width)
        for k in order
    ]
    both, at, found = (lax.all_gather(jnp.concatenate(lines), axis), 0, {})
    for k, line in zip(order, lines):
        slab = both[:, at : at + len(line)].reshape(len(both), -1)
        found[k] = slab[:, : leaves[k].size].reshape(-1, *leaves[k].shape)
        at += len(line)
    numbers = iter(range(len(leaves)))
    return jax.tree.map(lambda _: found[next(numbers)], value)


def combined_by_axis(value, axes, combine):
    for axis in axes:
        pieces = gathered_once(value, axis)
        value = jax.tree.map(lambda part: part[0], pieces)
        for k in range(1, lax.axis_size(axis)):
            value = combine(value, jax.tree.map(lambda part: part[k], pieces))
    return value


def fold_block(state, scores, value_rows):
    row_max, row_sum, weighted = state
    new_max = jnp.maximum(row_max, jnp.max(scores, axis=1))
    fading = jnp.exp(row_max - new_max)
    weights = jnp.exp(scores - new_max[:, None])
    row_sum = row_sum * fading + jnp.sum(weights, axis=1)
    weighted = weighted * fading[:, None] + jnp.dot(
        weights.astype(jnp.bfloat16), value_rows, preferred_element_type=jnp.float32
    )
    return (new_max, row_sum, weighted)


def partial_head(
    query_rows, cache_part, value_part, fresh_keys, fresh_values, first_token, span_total
):
    row_count = query_rows.shape[0]
    scaling = HD ** (-0.5)
    block_size = min(1024, cache_part.shape[0])
    block_count = cache_part.shape[0] // block_size
    key_blocks = cache_part.reshape(block_count, block_size, HD)
    value_blocks = value_part.reshape(block_count, block_size, HD)

    def advance(state, block_pair):
        scores = jnp.dot(query_rows, block_pair[0].T, preferred_element_type=jnp.float32) * scaling
        return (fold_block(state, scores, block_pair[1]), None)

    start_state = (
        jnp.full((row_count,), NEGATIVE, jnp.float32),
        jnp.zeros((row_count,), jnp.float32),
        jnp.zeros((row_count, HD), jnp.float32),
    )
    state, unused = lax.scan(advance, start_state, (key_blocks, value_blocks))
    scores = jnp.dot(query_rows, fresh_keys.T, preferred_element_type=jnp.float32) * scaling
    token_of_row = jnp.arange(row_count, dtype=jnp.int32) % span_total
    key_token = first_token + jnp.arange(fresh_keys.shape[0], dtype=jnp.int32)
    scores = jnp.where(token_of_row[:, None] >= key_token[None, :], scores, NEGATIVE)
    return fold_block(state, scores, fresh_values)


def combine_logits(first, second):
    row_max = jnp.maximum(first[0], second[0])
    row_sum = first[1] * jnp.exp(first[0] - row_max) + second[1] * jnp.exp(second[0] - row_max)
    return (row_max, row_sum, first[2] + second[2])


def local(
    queries,
    cache_keys,
    cache_values,
    span_keys,
    span_values,
    out_weight,
    residual,
    norm_gain,
    head_weight,
    targets,
    window_lengths,
):
    ctx_rank = lax.axis_index(CTX)
    span_dev = queries.shape[0]
    group_size = HEADS // KV_HEADS
    kv_local = cache_keys.shape[1] // HD
    heads_local = kv_local * group_size
    query_all = gathered_copies(queries, CTX, 0)
    span_total = query_all.shape[0]
    query_heads = (
        query_all.reshape(span_total, kv_local, group_size, HD)
        .transpose(1, 2, 0, 3)
        .reshape(kv_local, group_size * span_total, HD)
    )
    first_token = ctx_rank * span_dev
    row_max, row_sum, weighted = partial_head(
        query_heads[0], cache_keys, cache_values, span_keys, span_values, first_token, span_total
    )
    maxima = [row_max]
    totals = [row_sum]
    weighted_rows = [weighted]
    part_max = (
        jnp.stack(maxima)
        .reshape(kv_local, group_size, span_total)
        .transpose(2, 0, 1)
        .reshape(span_total, heads_local)
    )
    part_sum = (
        jnp.stack(totals)
        .reshape(kv_local, group_size, span_total)
        .transpose(2, 0, 1)
        .reshape(span_total, heads_local)
    )
    part_weighted = (
        jnp.stack(weighted_rows)
        .reshape(kv_local, group_size, span_total, HD)
        .transpose(2, 0, 1, 3)
        .reshape(span_total, heads_local * HD)
    )
    pieces = tuple(
        (
            part.astype(jnp.float32)
            for part in sent_together(
                (
                    part_max[None].astype(jnp.bfloat16),
                    part_sum[None].astype(jnp.bfloat16),
                    part_weighted[None].astype(jnp.bfloat16),
                ),
                CTX,
                1,
                0,
                2,
            )
        )
    )
    source_count = pieces[0].shape[0]
    row_max = jnp.max(pieces[0], axis=0)
    fading = jnp.exp(pieces[0] - row_max[None])
    row_sum = jnp.sum(pieces[1] * fading, axis=0)
    weighted = jnp.sum(
        pieces[2].reshape(source_count, span_dev, heads_local, HD) * fading[:, :, :, None], axis=0
    )
    attended_own = (
        (weighted / row_sum[:, :, None]).reshape(span_dev, heads_local * HD).astype(jnp.bfloat16)
    )
    attended_all = gathered_copies(attended_own, CTX, 0)
    projected = summed_on_arrival(
        jnp.dot(attended_all, out_weight, preferred_element_type=jnp.float32).astype(jnp.bfloat16),
        TP,
        0,
    )
    stream = residual.astype(jnp.float32) + projected
    squares = over_axes(jnp.sum(stream * stream, axis=1), CTX)
    scaled = lax.rsqrt(squares / D + EPSILON)
    normed_part = (stream * scaled[:, None] * norm_gain.astype(jnp.float32)[None, :]).astype(
        jnp.bfloat16
    )
    normed_rows = gathered_copies(normed_part, CTX, 1)
    logits = jnp.dot(
        lax.all_gather(normed_rows, TP, axis=0, tiled=True),
        head_weight,
        preferred_element_type=jnp.float32,
    )
    vocab_dev = head_weight.shape[1]
    vocab_start = lax.axis_index(CTX_TP) * vocab_dev
    columns = vocab_start + jnp.arange(vocab_dev, dtype=jnp.int32)
    target_part = jnp.sum(jnp.where(targets[:, None] == columns[None, :], logits, 0.0), axis=1)
    local_max = jnp.max(logits, axis=1)
    exp_part = jnp.sum(jnp.exp(logits - local_max[:, None]), axis=1)
    global_max, exp_total, target_logit = combined_by_axis(
        (local_max, exp_part, target_part), CTX_TP, combine_logits
    )
    token_logprob = target_logit - (global_max + jnp.log(exp_total))
    window_ends = jnp.cumsum(window_lengths)
    window_starts = window_ends - window_lengths
    positions = jnp.arange(span_total, dtype=jnp.int32)
    member = (
        (positions[None, :] >= window_starts[:, None]) & (positions[None, :] < window_ends[:, None])
    ).astype(jnp.float32)
    window_sums = jnp.dot(member, token_logprob)
    window_means = window_sums / window_lengths.astype(jnp.float32)
    own_logprob = lax.dynamic_slice_in_dim(token_logprob, first_token, span_dev, 0)
    return (own_logprob, window_means)


def solution(mesh):
    split = Mesh(mesh.devices.reshape(4, 4, 4, 2), ("ctx_0", "ctx_1", "tp_0", "tp_1"))
    in_specs = (
        P(CTX, TP),
        P(CTX, TP),
        P(CTX, TP),
        P(CTX, TP),
        P(CTX, TP),
        P(TP, CTX),
        P(TP, CTX),
        P(CTX),
        P(None, CTX_TP),
        P(),
        P(),
    )
    out_specs = (P(CTX), P())
    return jax.shard_map(local, mesh=split, in_specs=in_specs, out_specs=out_specs, check_vma=False)
```

profile of v0, /device:TPU:1, one launch (start us, length us, event | category | flops | bytes accessed | tf_op | source)
XLA Modules:
  0.0 373.4 jit_solution(12038084039484746735)
XLA Ops:
  9.3 8.5 %all-to-all-start = ((bf16[16,32,1024]{2,1,0:T(8,128)(2,1)}), bf16[16,32,1024]{2,1,0:T(8,128)(2,1)}, u32[]{:S(2)}, u32[]{:S(2)}) async-start(bf16[16,32,1024]{2,1,0:T(8,128)(2,1)} %broadcast_in_dim.24), calls=%async_computation | async-start | bytes 2097152 | tf_op jit(solution)/shard_map/all_to_all | solution.py:28
  17.8 15.7 %all-to-all-done = bf16[16,32,1024]{2,1,0:T(8,128)(2,1)} async-done(((bf16[16,32,1024]{2,1,0:T(8,128)(2,1)}), bf16[16,32,1024]{2,1,0:T(8,128)(2,1)}, u32[]{:S(2)}, u32[]{:S(2)}) %all-to-all-start) | async-done | bytes 1048608 | tf_op jit(solution)/shard_map/all_to_all | solution.py:28
  36.1 102.5 %while.15 = (s32[]{:T(128)}, f32[4096]{0:T(1024)S(1)}, f32[4096]{0:T(1024)S(1)}, f32[4096,128]{1,0:T(8,128)S(1)}, bf16[4,1024,128]{2,1,0:T(8,128)(2,1)}, /*index...) while((s32[]{:T(128)}, f32[4096]{0:T(1024)S(1)}, ...), condition=%wide.region_3.4_spmd.clone, body=%wide.region_0.3_spmd.clone.sunk | while | flops 2182631424 | bytes 56361076 | solution.py:127
  36.1 9.4 %multiply_reduce_fusion.5 = (f32[4096]{0:T(1024)S(1)}, f32[1024,4096]{1,0:T(8,128)}) fusion(bf16[4096,128]{1,0:T(8,128)(2,1)} %get-tuple-element.183, bf16[4,1024,128]{2,1,0:T(8,128)(2,1)} %get-tuple-element.182, s32[]{:T(128)S(6)} %copy.32), kind=kOutput, calls=%fused_computation.1.clone.1 | convolution fusion | flops 1082126336 | bytes 18104324 | tf_op jit(solution)/shard_map/while/body/eval_jaxpr/dot_general | solution.py:119
  45.5 8.5 %fusion.99 = f32[4096]{0:T(1024)S(1)} fusion(f32[1024,4096]{1,0:T(8,128)} %get-tuple-element.157, f32[4096]{0:T(1024)S(1)} %select_maximum_fusion.2), kind=kLoop, calls=%fused_computation.3.clone.1 | loop fusion | flops 12578816 | bytes 16809984 | tf_op jit(solution)/shard_map/while/body/eval_jaxpr/reduce_sum | solution.py:101
  54.1 7.7 %fusion.101 = f32[4096,128]{1,0:T(8,128)S(1)} fusion(f32[1024,4096]{1,0:T(8,128)} %get-tuple-element.157, f32[4096]{0:T(1024)S(1)} %select_maximum_fusion.2, f32[4096,128]{1,0:T(8,128)S(1)} %get-tuple-element.172, f32[4096]{0:T(1024)S(1)} %get-tuple-element.159, pred[]{:T(512)S(6)} %compare.4, bf16[4,1024,128]{2,1,0:T(8,128)(2,1)} %get-tuple-element.184, ...), kind=kOutput, calls=%fused_computation.7.clone.1 | convolution fusion | flops 1087897600 | bytes 21266436 | tf_op jit(solution)/shard_map/while/body/eval_jaxpr/dot_general | solution.py:102
  61.8 9.4 %multiply_reduce_fusion.5 = (f32[4096]{0:T(1024)S(1)}, f32[1024,4096]{1,0:T(8,128)}) fusion(bf16[4096,128]{1,0:T(8,128)(2,1)} %get-tuple-element.183, bf16[4,1024,128]{2,1,0:T(8,128)(2,1)} %get-tuple-element.182, s32[]{:T(128)S(6)} %copy.32), kind=kOutput, calls=%fused_computation.1.clone.1 | convolution fusion | flops 1082126336 | bytes 18104324 | tf_op jit(solution)/shard_map/while/body/eval_jaxpr/dot_general | solution.py:119
  71.1 8.5 %fusion.99 = f32[4096]{0:T(1024)S(1)} fusion(f32[1024,4096]{1,0:T(8,128)} %get-tuple-element.157, f32[4096]{0:T(1024)S(1)} %select_maximum_fusion.2), kind=kLoop, calls=%fused_computation.3.clone.1 | loop fusion | flops 12578816 | bytes 16809984 | tf_op jit(solution)/shard_map/while/body/eval_jaxpr/reduce_sum | solution.py:101
  87.4 9.4 %multiply_reduce_fusion.5 = (f32[4096]{0:T(1024)S(1)}, f32[1024,4096]{1,0:T(8,128)}) fusion(bf16[4096,128]{1,0:T(8,128)(2,1)} %get-tuple-element.183, bf16[4,1024,128]{2,1,0:T(8,128)(2,1)} %get-tuple-element.182, s32[]{:T(128)S(6)} %copy.32), kind=kOutput, calls=%fused_computation.1.clone.1 | convolution fusion | flops 1082126336 | bytes 18104324 | tf_op jit(solution)/shard_map/while/body/eval_jaxpr/dot_general | solution.py:119
  96.8 8.5 %fusion.99 = f32[4096]{0:T(1024)S(1)} fusion(f32[1024,4096]{1,0:T(8,128)} %get-tuple-element.157, f32[4096]{0:T(1024)S(1)} %select_maximum_fusion.2), kind=kLoop, calls=%fused_computation.3.clone.1 | loop fusion | flops 12578816 | bytes 16809984 | tf_op jit(solution)/shard_map/while/body/eval_jaxpr/reduce_sum | solution.py:101
  113.0 9.4 %multiply_reduce_fusion.5 = (f32[4096]{0:T(1024)S(1)}, f32[1024,4096]{1,0:T(8,128)}) fusion(bf16[4096,128]{1,0:T(8,128)(2,1)} %get-tuple-element.183, bf16[4,1024,128]{2,1,0:T(8,128)(2,1)} %get-tuple-element.182, s32[]{:T(128)S(6)} %copy.32), kind=kOutput, calls=%fused_computation.1.clone.1 | convolution fusion | flops 1082126336 | bytes 18104324 | tf_op jit(solution)/shard_map/while/body/eval_jaxpr/dot_general | solution.py:119
  122.4 8.5 %fusion.99 = f32[4096]{0:T(1024)S(1)} fusion(f32[1024,4096]{1,0:T(8,128)} %get-tuple-element.157, f32[4096]{0:T(1024)S(1)} %select_maximum_fusion.2), kind=kLoop, calls=%fused_computation.3.clone.1 | loop fusion | flops 12578816 | bytes 16809984 | tf_op jit(solution)/shard_map/while/body/eval_jaxpr/reduce_sum | solution.py:101
  150.8 9.2 %reduce.4 = bf16[512,1040]{1,0:T(8,128)(2,1)} reduce(bf16[512,1,1040]{2,1,0:T(2,128)(2,1)S(1)} %bitcast.306, bf16[]{:T(256)} %broadcast.82), dimensions={1}, to_apply=%bitcast.273.reduce_sub_computation | reduce | bytes 2129922
  163.8 18.9 %all_to_all.32 = bf16[16,2,16640]{2,1,0:T(2,128)(2,1)} all-to-all(bf16[16,2,16640]{2,1,0:T(2,128)(2,1)S(1)} %reshape.901), channel_id=1, replica_groups=mesh['ctx_0'=4,'ctx_1'=4,'tp_0'=4,'tp_1'=2] {'ctx_0','ctx_1'}, dimensions={0} | all-to-all | bytes 2129920 | tf_op jit(solution)/shard_map/all_to_all | solution.py:45
  194.5 16.1 %all_to_all.33 = bf16[16,32,1024]{2,1,0:T(8,128)(2,1)S(1)} all-to-all(bf16[16,32,1024]{2,1,0:T(8,128)(2,1)S(1)} %broadcast_in_dim.26), channel_id=1, replica_groups=mesh['ctx_0'=4,'ctx_1'=4,'tp_0'=4,'tp_1'=2] {'ctx_0','ctx_1'}, dimensions={0} | all-to-all | bytes 2097152 | tf_op jit(solution)/shard_map/all_to_all | solution.py:28
  212.1 9.2 %all-to-all-start.3 = ((bf16[8,64,512]{2,1,0:T(8,128)(2,1)}), bf16[8,64,512]{2,1,0:T(8,128)(2,1)S(1)}, u32[]{:S(2)}, u32[]{:S(2)}) async-start(bf16[8,64,512]{2,1,0:T(8,128)(2,1)} %bitcast.12), calls=%async_computation.3 | async-start | bytes 1048576 | tf_op jit(solution)/shard_map/all_to_all | solution.py:60
  221.3 9.3 %all-to-all-done.3 = bf16[8,64,512]{2,1,0:T(8,128)(2,1)S(1)} async-done(((bf16[8,64,512]{2,1,0:T(8,128)(2,1)}), bf16[8,64,512]{2,1,0:T(8,128)(2,1)S(1)}, u32[]{:S(2)}, u32[]{:S(2)}) %all-to-all-start.3) | async-done | bytes 524320 | tf_op jit(solution)/shard_map/all_to_all | solution.py:60
  244.2 15.1 %all_to_all.34 = bf16[16,64,512]{2,1,0:T(8,128)(2,1)S(1)} all-to-all(bf16[16,64,512]{2,1,0:T(8,128)(2,1)S(1)} %broadcast_in_dim.27), channel_id=1, replica_groups=mesh['ctx_0'=4,'ctx_1'=4,'tp_0'=4,'tp_1'=2] {'ctx_0','ctx_1'}, dimensions={0} | all-to-all | bytes 2097152 | tf_op jit(solution)/shard_map/all_to_all | solution.py:28
  260.7 51.3 %all-gather.10.cloned.1.call-done = bf16[512,8192]{1,0:T(8,128)(2,1)} async-done(((bf16[64,8192]{1,0:T(8,128)(2,1)}), bf16[512,8192]{1,0:T(8,128)(2,1)}) %all-gather.10.cloned.1.call-update) | async-done | bytes 8388624 | tf_op jit(solution)/shard_map/all_gather | solution.py:231
  312.0 14.2 %fusion.80 = (f32[512]{0:T(512)S(1)}, f32[512,1002]{0,1:T(8,128)S(1)}) fusion(bf16[512,8192]{1,0:T(8,128)(2,1)} %all-gather.10.cloned.1.call-done, bf16[8192,1002]{0,1:T(8,128)(2,1)} %param.21), kind=kOutput, calls=%fused_computation.145 | convolution fusion | flops 8405897728 | bytes 26859520 | tf_op jit(solution)/shard_map/dot_general | solution.py:230
  326.7 9.6 %all-gather.4 = f32[4,3,512]{2,1,0:T(4,128)S(1)} all-gather(f32[1,3,512]{2,1,0:T(4,128)S(1)} %maximum_bitcast_fusion), channel_id=2, replica_groups=mesh['ctx_0'=4,'ctx_1'=4,'tp_0'=4,'tp_1'=2] {'ctx_0'}, dimensions={0}, use_global_device_ids=true | all-gather | bytes 30720 | tf_op jit(solution)/shard_map/all_gather | solution.py:78
  336.4 9.5 %all-gather.5 = f32[4,3,512]{2,1,0:T(4,128)S(1)} all-gather(f32[1,3,512]{2,1,0:T(4,128)S(1)} %maximum_bitcast_fusion.1), channel_id=3, replica_groups=mesh['ctx_0'=4,'ctx_1'=4,'tp_0'=4,'tp_1'=2] {'ctx_1'}, dimensions={0}, use_global_device_ids=true | all-gather | bytes 30720 | tf_op jit(solution)/shard_map/all_gather | solution.py:78
  346.0 9.0 %all-gather.6 = f32[4,3,512]{2,1,0:T(4,128)S(1)} all-gather(f32[1,3,512]{2,1,0:T(4,128)S(1)} %maximum_bitcast_fusion.2), channel_id=4, replica_groups=mesh['ctx_0'=4,'ctx_1'=4,'tp_0'=4,'tp_1'=2] {'tp_0'}, dimensions={0}, use_global_device_ids=true | all-gather | bytes 30720 | tf_op jit(solution)/shard_map/all_gather | solution.py:78
  355.1 10.1 %all-gather.7 = f32[2,3,512]{2,1,0:T(4,128)S(1)} all-gather(f32[1,3,512]{2,1,0:T(4,128)S(1)} %maximum_bitcast_fusion.3), channel_id=5, replica_groups=mesh['ctx_0'=4,'ctx_1'=4,'tp_0'=4,'tp_1'=2] {'tp_1'}, dimensions={0}, use_global_device_ids=true | all-gather | bytes 18432 | tf_op jit(solution)/shard_map/all_gather | solution.py:78
  (92 shorter events, 73.8 us)
Async XLA Ops:
  7.2 203.5 %copy-start = (bf16[1024,512]{1,0:T(8,128)(2,1)S(1)}, bf16[1024,512]{1,0:T(8,128)(2,1)}, u32[]{:S(2)}) copy-start(bf16[1024,512]{1,0:T(8,128)(2,1)} %param.18) | copy-start | bytes 3145732
  9.3 24.2 %all-to-all-start = ((bf16[16,32,1024]{2,1,0:T(8,128)(2,1)}), bf16[16,32,1024]{2,1,0:T(8,128)(2,1)}, u32[]{:S(2)}, u32[]{:S(2)}) async-start(bf16[16,32,1024]{2,1,0:T(8,128)(2,1)} %broadcast_in_dim.24), calls=%async_computation | async-start | bytes 2097152 | tf_op jit(solution)/shard_map/all_to_all | solution.py:28
  36.1 102.5 %copy-start.3 = (bf16[32,128]{1,0:T(8,128)(2,1)S(1)}, bf16[32,128]{1,0:T(8,128)(2,1)}, u32[]{:S(2)}) copy-start(bf16[32,128]{1,0:T(8,128)(2,1)} %param.16) | copy-start | bytes 24580
  138.7 1.9 copy-start.4
  187.7 1.0 copy-start.1
  210.6 10.7 %copy-start.6 = (bf16[512]{0:T(512)(128)(2,1)S(1)}, bf16[512]{0:T(512)(128)(2,1)}, u32[]{:S(2)}) copy-start(bf16[512]{0:T(512)(128)(2,1)} %param.20) | copy-start | bytes 3076
  210.6 20.1 %copy-start.2 = (bf16[64,512]{1,0:T(8,128)(2,1)S(1)}, bf16[64,512]{1,0:T(8,128)(2,1)}, u32[]{:S(2)}) copy-start(bf16[64,512]{1,0:T(8,128)(2,1)} %param.19) | copy-start | bytes 196612
  212.1 18.5 %all-to-all-start.3 = ((bf16[8,64,512]{2,1,0:T(8,128)(2,1)}), bf16[8,64,512]{2,1,0:T(8,128)(2,1)S(1)}, u32[]{:S(2)}, u32[]{:S(2)}) async-start(bf16[8,64,512]{2,1,0:T(8,128)(2,1)} %bitcast.12), calls=%async_computation.3 | async-start | bytes 1048576 | tf_op jit(solution)/shard_map/all_to_all | solution.py:60
  221.3 90.7 %all-gather.10.cloned.1.call-start = ((), (), s32[]{:S(2)}) async-start(), calls=%async_computation.5 | async-start | bytes 9437184 | tf_op jit(solution)/shard_map/all_gather | solution.py:231
  259.3 1.2 copy-start.7
  260.7 65.5 %copy-start.5 = (s32[512]{0:T(512)S(1)}, s32[512]{0:T(512)}, u32[]{:S(2)}) copy-start(s32[512]{0:T(512)} %param.22) | copy-start | bytes 6148
Sparse Core Ops, SparseCore 0:
  260.6 51.3 all-gather.9
where the time goes:
time: 374 us; the launch traced here: 373 us
  blocking collectives  102 us (27%)
  matrix products  88.1 us (24%)
  waiting for transfers between devices  76.3 us (20%)
  other arithmetic  47.7 us (13%)
  local copies, waits for them, and re-layouts  27.5 us (7%)
  starting transfers between devices  17.6 us (5%)
  between operations  14.4 us (4%)
    all_gather x1, waiting for transfers between devices, local(): lax.all_gather(normed_rows, TP, axis=0, tiled=True)  51.3 us
    all_gather x4, blocking collectives, gathered_once(): both, at, found = (lax.all_gather(jnp.concatenate(lines), axis), 0, {})  38.3 us
    dot_general x4, matrix products, advance(): jnp.dot(query_rows, block_pair[0].T, preferred_element_type=jnp.float32)  37.5 us
    reduce_sum x5, other arithmetic, fold_block(): row_sum = row_sum * fading + jnp.sum(weights, axis=1)  34.2 us
    dot_general x5, matrix products, fold_block(): jnp.dot(weights.astype(jnp.bfloat16), value_rows, preferred_element_type=...  32.5 us
    all_to_all x2, blocking collectives, sent_to_all(): lax.all_to_all(jnp.broadcast_to(value[None], (count, *value.shape)), axis...  31.2 us
    all_to_all x1, blocking collectives, sent_together(): lax.all_to_all(both, axis, split_axis=split_dim, concat_axis=concat_dim,...  18.9 us
    all_to_all x1, waiting for transfers between devices, sent_to_all(): lax.all_to_all(jnp.broadcast_to(value[None], (count, *value.shape)), axis...  15.7 us
  transfers between devices with their start and end apart: 3, of which 3 were waited for; matrix products, arithmetic and copies ran while one was open for 0% of the time, Pallas kernels for 0%

commit v1 on v0

v1 whole, which is shorter than its diff:
```python
import jax
import jax.numpy as jnp
from jax import lax
from jax.experimental import pallas as pl
from jax.experimental.pallas import tpu as pltpu
from jax.sharding import Mesh
from jax.sharding import PartitionSpec as P

D = 8192
HEADS = 64
KV_HEADS = 8
HD = 128
GROUP = HEADS // KV_HEADS
CTX = ("ctx_0", "ctx_1")
TP = ("tp_0", "tp_1")
CTX_TP = ("ctx_0", "ctx_1", "tp_0", "tp_1")
EPSILON = 1e-05
NEGATIVE = -1e30
LOG2E = 1.4426950408889634
TO_LOG2 = HD ** (-0.5) * LOG2E
ROWS = 256
KEYS = 2048


def sent_to_all(value, axis):
    count = lax.axis_size(axis)
    return lax.all_to_all(
        jnp.broadcast_to(value[None], (count, *value.shape)), axis, 0, 0, tiled=True
    )


def whole(*shape):
    return pl.BlockSpec(shape, lambda *at: (0,) * len(shape))


def attend(first_token, queries, keys, values, fresh_keys, fresh_values, side):
    sources, span_dev, width = queries.shape
    span, cached, fresh = sources * span_dev, keys.shape[0], fresh_keys.shape[0]
    heads = width // HD
    total = cached + 128
    chunks = [(a, KEYS) for a in range(0, cached, KEYS)]
    chunks[-1] = (chunks[-1][0], total - chunks[-1][0])

    def body(first_ref, q_ref, k_ref, v_ref, fk_ref, fv_ref, side_ref, out_ref, kt, va, sbuf, mbuf):
        i = pl.program_id(0)

        @pl.when(i == 0)
        def _():
            for a in range(0, cached, 512):
                kt[:, a : a + 512] = k_ref[a : a + 512, :].T
            gap = jnp.zeros((128 - fresh, HD), jnp.bfloat16)
            kt[:, cached:] = jnp.concatenate([fk_ref[...], gap], 0).T
            va[:cached, :HD] = v_ref[...]
            va[cached:, :HD] = jnp.concatenate([fv_ref[...], gap], 0)
            va[:, HD:] = jnp.ones((total, HD), jnp.bfloat16)
            out_ref[:, :, width:] = jnp.broadcast_to(side_ref[...], (sources, span_dev, HD))

        def step(scoring, weighing):
            to = lax.rem(i, 2)
            at = lax.rem(i + 1, 2)
            for r in range(0, span, ROWS):
                rows = slice(r, r + ROWS)
                tokens = slice(r // span_dev, (r + ROWS) // span_dev)
                top, acc = None, None
                if scoring:
                    q = q_ref[tokens].reshape(ROWS, HD)
                if weighing:
                    shift = mbuf[at, rows, :]
                for a, n in chunks:
                    if scoring:
                        s = jnp.dot(q, kt[:, a : a + n], preferred_element_type=jnp.float32)
                        if a + n == total:
                            col = lax.broadcasted_iota(jnp.int32, (ROWS, 128), 1)
                            row = lax.broadcasted_iota(jnp.int32, (ROWS, 128), 0) + r
                            seen = (col < fresh) & (row >= col + first_ref[0])
                            tail = jnp.where(seen, s[:, n - 128 :], NEGATIVE)
                            s = jnp.concatenate([s[:, : n - 128], tail], 1)
                        sbuf[to, rows, a : a + n] = s
                        for b in range(0, n, 128):
                            piece = s[:, b : b + 128]
                            top = piece if top is None else jnp.maximum(top, piece)
                    if weighing:
                        p = jnp.concatenate(
                            [
                                jnp.exp2(
                                    sbuf[at, rows, a + b : a + b + 128] * TO_LOG2 - shift
                                ).astype(jnp.bfloat16)
                                for b in range(0, n, 128)
                            ],
                            1,
                        )
                        d = jnp.dot(p, va[a : a + n, :], preferred_element_type=jnp.float32)
                        acc = d if acc is None else acc + d
                if scoring:
                    m = jnp.max(top, axis=1, keepdims=True) * TO_LOG2
                    mbuf[to, rows, :] = jnp.broadcast_to(m, (ROWS, 128))
                if weighing:
                    h = i - 1
                    row_sum = acc[:, HD:]
                    o = (acc[:, :HD] / row_sum).astype(jnp.bfloat16)
                    place = pl.ds(pl.multiple_of(h * HD, HD), HD)
                    out_ref[tokens, :, place] = o.reshape(-1, span_dev, HD)
                    level = shift + jnp.log2(row_sum)
                    high = level.astype(jnp.bfloat16).astype(jnp.float32)
                    low = level - high
                    lane = lax.broadcasted_iota(jnp.int32, (ROWS, HD), 1)
                    old = out_ref[tokens, :, width:].reshape(ROWS, HD).astype(jnp.float32)
                    new = jnp.where(lane == h, high, jnp.where(lane == h + heads, low, old))
                    out_ref[tokens, :, width:] = new.astype(jnp.bfloat16).reshape(-1, span_dev, HD)

        @pl.when(i == 0)
        def _():
            step(True, False)

        @pl.when((i > 0) & (i < heads))
        def _():
            step(True, True)

        @pl.when(i == heads)
        def _():
            step(False, True)

    out_shape = (sources, span_dev, width + HD)
    return pl.pallas_call(
        body,
        out_shape=jax.ShapeDtypeStruct(out_shape, jnp.bfloat16),
        grid_spec=pltpu.PrefetchScalarGridSpec(
            num_scalar_prefetch=1,
            grid=(heads + 1,),
            in_specs=[
                pl.BlockSpec(
                    (sources, span_dev, HD), lambda i, f: (0, 0, jnp.minimum(i, heads - 1))
                ),
                whole(cached, HD),
                whole(cached, HD),
                whole(fresh, HD),
                whole(fresh, HD),
                whole(1, span_dev, HD),
            ],
            out_specs=whole(*out_shape),
            scratch_shapes=[
                pltpu.VMEM((HD, total), jnp.bfloat16),
                pltpu.VMEM((total, 2 * HD), jnp.bfloat16),
                pltpu.VMEM((2, span, total), jnp.float32),
                pltpu.VMEM((2, span, HD), jnp.float32),
            ],
        ),
        compiler_params=pltpu.CompilerParams(
            dimension_semantics=("arbitrary",), vmem_limit_bytes=48 << 20
        ),
        cost_estimate=pl.CostEstimate(
            flops=4 * heads * span * total * HD,
            transcendentals=heads * span * total,
            bytes_accessed=6 << 20,
        ),
        name="attend",
    )(first_token, queries, keys, values, fresh_keys, fresh_values, side)


def merge(pieces, copies):
    sources, span_dev, wide = pieces.shape
    width = wide - HD
    heads = width // HD

    def body(in_ref, out_ref):
        tail = in_ref[:, :, width:].astype(jnp.float32).reshape(sources * span_dev, HD)
        level = (tail + pltpu.roll(tail, HD - heads, 1)).reshape(sources, span_dev, HD)
        top = jnp.max(level, axis=0)
        weight = jnp.exp2(level - top[None])
        weight = weight / jnp.sum(weight, axis=0)[None]
        for h in range(heads):
            cols = slice(h * HD, (h + 1) * HD)
            acc = None
            for k in range(sources):
                part = in_ref[k, :, cols].astype(jnp.float32) * weight[k][:, h : h + 1]
                acc = part if acc is None else acc + part
            acc = acc.astype(jnp.bfloat16)
            for k in range(copies):
                out_ref[k, :, cols] = acc

    return pl.pallas_call(
        body,
        out_shape=jax.ShapeDtypeStruct((copies, span_dev, width), jnp.bfloat16),
        in_specs=[whole(*pieces.shape)],
        out_specs=whole(copies, span_dev, width),
        grid=(1,),
        name="merge",
    )(pieces)


def score(rows, inverse, weight, local_target):
    tps, parts, tokens, cols = rows.shape
    span = tps * tokens
    vocab = weight.shape[1]
    per = 2
    steps = parts // per

    def body(x_ref, inv_ref, w_ref, t_ref, out_ref, acc, squares):
        i = pl.program_id(0)
        total, ss = None, None
        for k in range(per):
            x = x_ref[:, k].reshape(span, cols)
            d = jnp.dot(x, w_ref[k * cols : (k + 1) * cols, :], preferred_element_type=jnp.float32)
            total = d if total is None else total + d
            xf = x.astype(jnp.float32)
            sq = xf * xf * inv_ref[k]
            for b in range(0, cols, 128):
                piece = sq[:, b : b + 128]
                ss = piece if ss is None else ss + piece

        @pl.when(i == 0)
        def _():
            acc[...] = total
            squares[...] = ss

        @pl.when(i > 0)
        def _():
            acc[...] += total
            squares[...] += ss

        @pl.when(i == steps - 1)
        def _():
            mean = jnp.sum(squares[...], axis=1, keepdims=True) / D
            logits = acc[...] * lax.rsqrt(mean + EPSILON)
            col = lax.broadcasted_iota(jnp.int32, (span, vocab), 1)
            top = jnp.max(logits, axis=1, keepdims=True)
            sums = jnp.sum(jnp.exp(logits - top), axis=1, keepdims=True)
            level = top + jnp.log(sums)
            hit = jnp.sum(jnp.where(col == t_ref[...], logits, 0.0), axis=1, keepdims=True)
            lane = lax.broadcasted_iota(jnp.int32, (span, 128), 1)
            both = jnp.where(lane == 0, level, hit)
            out_ref[...] = both.T[:2, :]

    return pl.pallas_call(
        body,
        out_shape=jax.ShapeDtypeStruct((2, span), jnp.float32),
        grid=(steps,),
        in_specs=[
            pl.BlockSpec((tps, per, tokens, cols), lambda i: (0, i, 0, 0)),
            pl.BlockSpec((per, 1, cols), lambda i: (i, 0, 0)),
            pl.BlockSpec((per * cols, vocab), lambda i: (i, 0)),
            whole(span, 1),
        ],
        out_specs=whole(2, span),
        scratch_shapes=[
            pltpu.VMEM((span, vocab), jnp.float32),
            pltpu.VMEM((span, 128), jnp.float32),
        ],
        compiler_params=pltpu.CompilerParams(
            dimension_semantics=("arbitrary",), vmem_limit_bytes=48 << 20
        ),
        cost_estimate=pl.CostEstimate(
            flops=2 * span * D * vocab, transcendentals=span * vocab, bytes_accessed=26 << 20
        ),
        name="score",
    )(rows, inverse, weight, local_target)


def joined(level_hit, axis):
    pieces = sent_to_all(level_hit, axis)
    level, hit = pieces[:, 0], pieces[:, 1]
    top = jnp.max(level, axis=0)
    total = top + jnp.log(jnp.sum(jnp.exp(level - top[None]), axis=0))
    return jnp.stack([total, jnp.sum(hit, axis=0)])


def local(
    queries,
    cache_keys,
    cache_values,
    span_keys,
    span_values,
    out_weight,
    residual,
    norm_gain,
    head_weight,
    targets,
    window_lengths,
):
    ctx_rank = lax.axis_index(CTX)
    span_dev, width = queries.shape
    ctx_size, tp_size = lax.axis_size(CTX), lax.axis_size(TP)
    span_total = span_dev * ctx_size
    first_token = ctx_rank * span_dev
    model_dev = norm_gain.shape[0]
    gain_lanes = model_dev // span_dev
    side = jnp.pad(
        norm_gain.reshape(1, span_dev, gain_lanes),
        ((0, 0), (0, 0), (2 * GROUP, HD - 2 * GROUP - gain_lanes)),
    )
    partial = attend(
        first_token.reshape(1),
        sent_to_all(queries, CTX),
        cache_keys,
        cache_values,
        span_keys,
        span_values,
        side,
    )
    pieces = lax.all_to_all(partial, CTX, split_axis=0, concat_axis=0, tiled=True)
    gains = pieces[:, :, width + 2 * GROUP : width + 2 * GROUP + gain_lanes]
    gains = gains.reshape(ctx_size, 1, model_dev).astype(jnp.float32)
    inverse = 1.0 / (gains * gains)
    attended = lax.all_to_all(merge(pieces, ctx_size), CTX, split_axis=0, concat_axis=0, tiled=True)
    projected = jnp.dot(
        attended.reshape(span_total, width), out_weight, preferred_element_type=jnp.float32
    ).astype(jnp.bfloat16)
    arrived = lax.all_to_all(
        projected.reshape(tp_size, span_total // tp_size, model_dev), TP, 0, 0, tiled=True
    )
    stream = residual.astype(jnp.float32) + arrived.astype(jnp.float32).sum(axis=0)
    gained = (stream * norm_gain.astype(jnp.float32)[None, :]).astype(jnp.bfloat16)
    rows = lax.all_gather(sent_to_all(gained, CTX), TP)
    vocab_dev = head_weight.shape[1]
    local_target = (targets - lax.axis_index(CTX_TP) * vocab_dev).reshape(span_total, 1)
    level_hit = score(rows, inverse, head_weight, local_target)
    level_hit = joined(joined(level_hit, CTX), TP)
    token_logprob = level_hit[1] - level_hit[0]
    window_ends = jnp.cumsum(window_lengths)
    window_starts = window_ends - window_lengths
    positions = jnp.arange(span_total, dtype=jnp.int32)
    member = (positions[None, :] >= window_starts[:, None]) & (
        positions[None, :] < window_ends[:, None]
    )
    window_sums = jnp.sum(jnp.where(member, token_logprob[None, :], 0.0), axis=1)
    window_means = window_sums / window_lengths.astype(jnp.float32)
    own_logprob = lax.dynamic_slice_in_dim(token_logprob, first_token, span_dev, 0)
    return (own_logprob, window_means)


def solution(mesh):
    split = Mesh(mesh.devices.reshape(4, 4, 4, 2), ("ctx_0", "ctx_1", "tp_0", "tp_1"))
    in_specs = (
        P(CTX, TP),
        P(CTX, TP),
        P(CTX, TP),
        P(CTX, TP),
        P(CTX, TP),
        P(TP, CTX),
        P(TP, CTX),
        P(CTX),
        P(None, CTX_TP),
        P(),
        P(),
    )
    out_specs = (P(CTX), P())
    return jax.shard_map(local, mesh=split, in_specs=in_specs, out_specs=out_specs, check_vma=False)
```

time: 374 us -> 239 us (0.64)
  matrix products: 88.1 us -> 1.5 us
  blocking collectives: 102 us -> 55.7 us
  other arithmetic: 47.7 us -> 2.22 us
  Pallas kernels: 0 us -> 44.3 us
  waiting for transfers between devices: 76.3 us -> 59.2 us
  starting transfers between devices: 17.6 us -> 29.2 us
  local copies, waits for them, and re-layouts: 27.5 us -> 31.5 us
    dot_general x13 -> x1, matrix products: 88.1 us -> 1.5 us  [local(): jnp.dot(attended.reshape(span_total, width), out_weight, preferred_elemen...]
    pallas_call x0 -> x3, Pallas kernels: none -> 44.3 us  [the longest x1 24.8 us: attend(): pl.pallas_call(body, out_shape=jax.ShapeDtypeStruct(out_shape, jnp.bfloat...]
    all_gather x4 -> x0, blocking collectives: 38.3 us -> none  [gathered_once(): both, at, found = (lax.all_gather(jnp.concatenate(lines), axis), 0, {})]
    reduce_sum x10 -> x4, other arithmetic: 36.8 us -> 0.31 us  [the longest x1 0.19 us: local(): jnp.sum(jnp.where(member, token_logprob[None, :], 0.0), axis=1)]
    all_gather x1, waiting for transfers between devices: 51.3 us -> 24 us  [local(): rows = lax.all_gather(sent_to_all(gained, CTX), TP)]
    all_to_all x1 -> x2, blocking collectives: 18.9 us -> 36.6 us  [the longest x1 19.6 us: local(): lax.all_to_all(partial, CTX, split_axis=0, concat_axis=0, tiled=True)]
    unnamed x21 -> x19, local copies, waits for them, and re-layouts: 11.7 us -> 26.4 us
    psum x2 -> x0, blocking collectives: 13.2 us -> none  [over_axes(): value = lax.psum(value, axis)]
  transfers between devices with their start and end apart: 3 -> 5, of which waited for: 3 -> 5; matrix products, arithmetic and copies ran while one was open for 0% -> 10% of each run, Pallas kernels for 0% -> 0%
where the time goes in v1:
time: 239 us; the launch traced here: 238 us
  waiting for transfers between devices  59.2 us (25%)
  blocking collectives  55.7 us (23%)
  Pallas kernels  44.3 us (19%)
  local copies, waits for them, and re-layouts  31.5 us (13%)
  starting transfers between devices  29.2 us (12%)
  between operations  14.2 us (6%)
    unnamed x19, local copies, waits for them, and re-layouts  26.4 us
    all_to_all x3, waiting for transfers between devices, sent_to_all(): lax.all_to_all(jnp.broadcast_to(value[None], (count, *value.shape)), axis...  25.9 us
    pallas_call x1, Pallas kernels, attend(): pl.pallas_call(body, out_shape=jax.ShapeDtypeStruct(out_shape, jnp.bfloat...  24.8 us
    all_gather x1, waiting for transfers between devices, local(): rows = lax.all_gather(sent_to_all(gained, CTX), TP)  24 us
    all_to_all x3, starting transfers between devices, sent_to_all(): lax.all_to_all(jnp.broadcast_to(value[None], (count, *value.shape)), axis...  20 us
    all_to_all x1, blocking collectives, local(): lax.all_to_all(partial, CTX, split_axis=0, concat_axis=0, tiled=True)  19.6 us
    all_to_all x1, blocking collectives, sent_to_all(): lax.all_to_all(jnp.broadcast_to(value[None], (count, *value.shape)), axis...  19.1 us
    all_to_all x1, blocking collectives, local(): lax.all_to_all(merge(pieces, ctx_size), CTX, split_axis=0, concat_axis=0,...  17 us
  transfers between devices with their start and end apart: 5, of which 5 were waited for; matrix products, arithmetic and copies ran while one was open for 10% of the time, Pallas kernels for 0%

profile of v1, /device:TPU:1, one launch (start us, length us, event | category | flops | bytes accessed | tf_op | source)
XLA Modules:
  0.0 237.8 jit_solution(3384176857167786394)
XLA Ops:
  7.2 2.0 broadcast_in_dim.16
  9.2 8.4 %all-to-all-start = ((bf16[16,32,1024]{2,1,0:T(8,128)(2,1)}), bf16[16,32,1024]{2,1,0:T(8,128)(2,1)S(1)}, u32[]{:S(2)}, u32[]{:S(2)}) async-start(bf16[16,32,1024]{2,1,0:T(8,128)(2,1)} %broadcast_in_dim.16), calls=%async_computation | async-start | bytes 2097152 | tf_op jit(solution)/shard_map/all_to_all | solution.py:27
  17.7 0.8 reshape.100
  18.5 14.8 %all-to-all-done.q_ref = bf16[16,32,1024]{2,1,0:T(8,128)(2,1)S(1)} async-done(((bf16[16,32,1024]{2,1,0:T(8,128)(2,1)}), bf16[16,32,1024]{2,1,0:T(8,128)(2,1)S(1)}, u32[]{:S(2)}, u32[]{:S(2)}) %all-to-all-start) | async-done | bytes 1048608 | tf_op jit(solution)/shard_map/all_to_all | solution.py:27
  33.3 1.2 copy-done.1
  34.5 1.2 copy-done.2
  35.8 0.7 copy-done.3
  36.5 0.7 copy-done.4
  37.2 24.8 %attend.1 = bf16[16,32,1152]{2,1,0:T(8,128)(2,1)S(1)} custom-call(s32[1]{0:T(128)} %bitcast.first_ref, bf16[16,32,1024]{2,1,0:T(8,128)(2,1)S(1)} %all-to-all-done.q_ref, bf16[4096,128]{1,0:T(8,128)(2,1)S(1)} %copy-done.1, bf16[4096,128]{1,0:T(8,128)(2,1)S(1)} %copy-done.2, bf16[32,128]{1,0:T(8,128)(2,1)S(1)} %copy-done.3, bf16[32,128]{1,0:T(8,128)(2,1)S(1)} %copy-done.4, ...), custom_call_target="tpu_custom_call" | custom-call | flops 8858370048 | bytes 6291456 | tf_op jit(solution)/shard_map/attend/pallas_call | solution.py:124
  62.0 19.6 %all_to_all.35.in_ref = bf16[16,32,1152]{2,1,0:T(8,128)(2,1)} all-to-all(bf16[16,32,1152]{2,1,0:T(8,128)(2,1)S(1)} %attend.1), channel_id=1, replica_groups=mesh['ctx_0'=4,'ctx_1'=4,'tp_0'=4,'tp_1'=2] {'ctx_0','ctx_1'}, dimensions={0} | all-to-all | bytes 2359296 | tf_op jit(solution)/shard_map/all_to_all | solution.py:300
  81.5 3.2 %merge.1 = bf16[16,32,1024]{2,1,0:T(8,128)(2,1)} custom-call(bf16[16,32,1152]{2,1,0:T(8,128)(2,1)} %all_to_all.35.in_ref), custom_call_target="tpu_custom_call" | custom-call | tf_op jit(solution)/shard_map/merge/pallas_call | solution.py:181
  84.7 17.0 %all_to_all.36 = bf16[16,32,1024]{2,1,0:T(8,128)(2,1)S(1)} all-to-all(bf16[16,32,1024]{2,1,0:T(8,128)(2,1)} %merge.1), channel_id=1, replica_groups=mesh['ctx_0'=4,'ctx_1'=4,'tp_0'=4,'tp_1'=2] {'ctx_0','ctx_1'}, dimensions={0} | all-to-all | bytes 2097152 | tf_op jit(solution)/shard_map/all_to_all | solution.py:304
  101.7 1.5 convolution_convert_fusion
  103.2 9.2 %all-to-all-start.3 = ((bf16[8,64,512]{2,1,0:T(8,128)(2,1)}), bf16[8,64,512]{2,1,0:T(8,128)(2,1)S(1)}, u32[]{:S(2)}, u32[]{:S(2)}) async-start(bf16[8,64,512]{2,1,0:T(8,128)(2,1)} %bitcast.2), calls=%async_computation.3 | async-start | bytes 1048576 | tf_op jit(solution)/shard_map/all_to_all | solution.py:308
  112.4 9.3 %all-to-all-done.3 = bf16[8,64,512]{2,1,0:T(8,128)(2,1)S(1)} async-done(((bf16[8,64,512]{2,1,0:T(8,128)(2,1)}), bf16[8,64,512]{2,1,0:T(8,128)(2,1)S(1)}, u32[]{:S(2)}, u32[]{:S(2)}) %all-to-all-start.3) | async-done | bytes 524320 | tf_op jit(solution)/shard_map/all_to_all | solution.py:308
  122.0 19.1 %all_to_all.37 = bf16[16,64,512]{2,1,0:T(8,128)(2,1)} all-to-all(bf16[16,64,512]{2,1,0:T(8,128)(2,1)S(1)} %broadcast_in_dim.17), channel_id=1, replica_groups=mesh['ctx_0'=4,'ctx_1'=4,'tp_0'=4,'tp_1'=2] {'ctx_0','ctx_1'}, dimensions={0} | all-to-all | bytes 2097152 | tf_op jit(solution)/shard_map/all_to_all | solution.py:27
  141.3 22.5 %copy.24.w_ref = bf16[8192,1002]{1,0:T(8,128)(2,1)} copy(bf16[8192,1002]{0,1:T(8,128)(2,1)} %param.19) | data formatting | bytes 32833536 | tf_op args[8]
  163.9 1.0 multiply_divide_fusion
  165.0 24.0 %all-gather.3.cloned.1.call-done = bf16[128,64,512]{2,1,0:T(8,128)(2,1)} async-done(((bf16[16,64,512]{2,1,0:T(8,128)(2,1)}), bf16[128,64,512]{2,1,0:T(8,128)(2,1)}) %all-gather.3.cloned.1.call-update) | async-done | bytes 8388624 | tf_op jit(solution)/shard_map/all_gather | solution.py:313
  189.0 16.3 %score.1 = f32[2,512]{1,0:T(2,128)S(1)} custom-call(bf16[8,16,64,512]{3,2,1,0:T(8,128)(2,1)} %bitcast.29, f32[16,1,512]{2,1,0:T(1,128)S(1)} %div.15.inv_ref, bf16[8192,1002]{1,0:T(8,128)(2,1)} %copy.24.w_ref, s32[512,1]{1,0:T(8,128)S(1)} %copy.25.t_ref), custom_call_target="tpu_custom_call" | custom-call | flops 8405385216 | bytes 27262976 | tf_op jit(solution)/shard_map/score/pallas_call | solution.py:234
  206.0 6.7 %all-to-all-start.5 = ((f32[16,2,512]{2,1,0:T(2,128)}), f32[16,2,512]{2,1,0:T(2,128)S(1)}, u32[]{:S(2)}, u32[]{:S(2)}) async-start(f32[16,2,512]{2,1,0:T(2,128)} %broadcast_in_dim.18), calls=%async_computation.5 | async-start | bytes 131072 | tf_op jit(solution)/shard_map/all_to_all | solution.py:27
  212.8 6.3 %all-to-all-done.5 = f32[16,2,512]{2,1,0:T(2,128)S(1)} async-done(((f32[16,2,512]{2,1,0:T(2,128)}), f32[16,2,512]{2,1,0:T(2,128)S(1)}, u32[]{:S(2)}, u32[]{:S(2)}) %all-to-all-start.5) | async-done | bytes 65568 | tf_op jit(solution)/shard_map/all_to_all | solution.py:27
  219.9 4.9 %all-to-all-start.6 = ((f32[8,2,512]{2,1,0:T(2,128)}), f32[8,2,512]{2,1,0:T(2,128)S(1)}, u32[]{:S(2)}, u32[]{:S(2)}) async-start(f32[8,2,512]{2,1,0:T(2,128)} %broadcast_in_dim.19), calls=%async_computation.6 | async-start | bytes 65536 | tf_op jit(solution)/shard_map/all_to_all | solution.py:27
  224.8 4.7 %all-to-all-done.6 = f32[8,2,512]{2,1,0:T(2,128)S(1)} async-done(((f32[8,2,512]{2,1,0:T(2,128)}), f32[8,2,512]{2,1,0:T(2,128)S(1)}, u32[]{:S(2)}, u32[]{:S(2)}) %all-to-all-start.6) | async-done | bytes 32800 | tf_op jit(solution)/shard_map/all_to_all | solution.py:27
  (38 shorter events, 3.6 us)
Async XLA Ops:
  7.2 94.6 %copy-start = (bf16[1024,512]{1,0:T(8,128)(2,1)S(1)}, bf16[1024,512]{1,0:T(8,128)(2,1)}, u32[]{:S(2)}) copy-start(bf16[1024,512]{1,0:T(8,128)(2,1)} %param.16) | copy-start | bytes 3145732
  9.2 24.1 %all-to-all-start = ((bf16[16,32,1024]{2,1,0:T(8,128)(2,1)}), bf16[16,32,1024]{2,1,0:T(8,128)(2,1)S(1)}, u32[]{:S(2)}, u32[]{:S(2)}) async-start(bf16[16,32,1024]{2,1,0:T(8,128)(2,1)} %broadcast_in_dim.16), calls=%async_computation | async-start | bytes 2097152 | tf_op jit(solution)/shard_map/all_to_all | solution.py:27
  33.3 1.2 copy-start.1
  34.5 1.2 copy-start.2
  35.8 0.7 copy-start.3
  36.5 0.7 copy-start.4
  61.9 50.5 %copy-start.6 = (bf16[512]{0:T(512)(128)(2,1)S(1)}, bf16[512]{0:T(512)(128)(2,1)}, u32[]{:S(2)}) copy-start(bf16[512]{0:T(512)(128)(2,1)} %param.18) | copy-start | bytes 3076
  61.9 59.9 %copy-start.5 = (bf16[64,512]{1,0:T(8,128)(2,1)S(1)}, bf16[64,512]{1,0:T(8,128)(2,1)}, u32[]{:S(2)}) copy-start(bf16[64,512]{1,0:T(8,128)(2,1)} %param.17) | copy-start | bytes 196612
  61.9 79.2 %copy-start.7 = (s32[512]{0:T(512)S(1)}, s32[512]{0:T(512)}, u32[]{:S(2)}) copy-start(s32[512]{0:T(512)} %param.20) | copy-start | bytes 6148
  103.2 18.5 %all-to-all-start.3 = ((bf16[8,64,512]{2,1,0:T(8,128)(2,1)}), bf16[8,64,512]{2,1,0:T(8,128)(2,1)S(1)}, u32[]{:S(2)}, u32[]{:S(2)}) async-start(bf16[8,64,512]{2,1,0:T(8,128)(2,1)} %bitcast.2), calls=%async_computation.3 | async-start | bytes 1048576 | tf_op jit(solution)/shard_map/all_to_all | solution.py:308
  112.4 76.6 %all-gather.3.cloned.1.call-start = ((), (), s32[]{:S(2)}) async-start(), calls=%async_computation.7 | async-start | bytes 9437184 | tf_op jit(solution)/shard_map/all_gather | solution.py:313
  189.0 23.7 %copy-start.8 = (s32[8]{0:T(128)S(1)}, s32[8]{0:T(128)}, u32[]{:S(2)}) copy-start(s32[8]{0:T(128)} %param.21) | copy-start | bytes 100
  206.0 13.2 %all-to-all-start.5 = ((f32[16,2,512]{2,1,0:T(2,128)}), f32[16,2,512]{2,1,0:T(2,128)S(1)}, u32[]{:S(2)}, u32[]{:S(2)}) async-start(f32[16,2,512]{2,1,0:T(2,128)} %broadcast_in_dim.18), calls=%async_computation.5 | async-start | bytes 131072 | tf_op jit(solution)/shard_map/all_to_all | solution.py:27
  219.9 9.7 %all-to-all-start.6 = ((f32[8,2,512]{2,1,0:T(2,128)}), f32[8,2,512]{2,1,0:T(2,128)S(1)}, u32[]{:S(2)}, u32[]{:S(2)}) async-start(f32[8,2,512]{2,1,0:T(2,128)} %broadcast_in_dim.19), calls=%async_computation.6 | async-start | bytes 65536 | tf_op jit(solution)/shard_map/all_to_all | solution.py:27
Sparse Core Ops, SparseCore 0:
  141.2 47.6 all-gather.2
